TPU v7x, 32 devices: a whole 2x2x4 slice. The times are simulated.
32 devices in a mesh: elem: 16 (over z, y, x), param: 2 (over core).
Axes of the slice: x: 2, y: 2, z: 4, core: 2. Of those that a mesh axis runs over, the one named last changes fastest.
Arguments:
- coords: bfloat16 [8, 300], P('param'), may hold values from -6 to 6
- basis_rows: bfloat16 [3, 300, 4096], P(None, None, 'elem'), may hold values from -0.375 to 0.375
- connectivity: int32 [4096, 8], P(('elem', 'param')), may hold values from 0 to 319, as said below
- modulus: float32 [4096], P(('elem', 'param')), may hold values from 0.5 to 15
- stiffness: float32 [24, 24], replicated, may hold values from -1.25 to 1.25
Outputs:
- training: bfloat16 [8, 300, 4096], P(None, None, ('elem', 'param'))
- target: float32 [8, 300], replicated
Inputs may be any that keep to these rules, and one draw needn't show every extreme that they name: `connectivity`: A number c of 256 or more names node c - 256 of the next node block; the last block's next block is the first. An element's eight corner numbers lie among min(8, 64) consecutive numbers; where these lie in the block is not tied to the element's position.
All inputs are finite; a program needn't handle non-finite values.
Results may differ from a plain program's by a relative error of at most 0.0072.
Values may be sent and summed in bfloat16 or wider, within the bound.
A program may use at most 64 MiB of HBM per device.

v0:
```python
import math
import jax
import jax.numpy as jnp
from jax import lax
from jax.sharding import PartitionSpec as P


def passed_along(value, axis, by):
    peers = lax.axis_size(axis)
    return lax.ppermute(value, axis, [(i, (i + by) % peers) for i in range(peers)])


def local(coords, basis_rows, connectivity, modulus, stiffness):
    node_count = basis_rows.shape[2]
    ghost_count = node_count // 4
    ghost_rows = passed_along(basis_rows[:, :, :ghost_count], "elem", -1)
    extended = jnp.concatenate([basis_rows, ghost_rows], axis=2)
    corner_ids = connectivity.T
    elem_count = corner_ids.shape[1]
    element_basis = extended[:, :, corner_ids]
    cycle_size = lax.axis_size("param")
    all_coords = lax.all_gather(coords, "param", axis=0, tiled=True)
    displaced = jnp.stack(
        [
            jnp.dot(all_coords, extended[component], preferred_element_type=jnp.float32)
            for component in range(3)
        ],
        axis=1,
    ).astype(jnp.bfloat16)
    snaps = displaced.shape[0]
    corner_disp = displaced[:, :, corner_ids].reshape(snaps, 24, elem_count).astype(jnp.float32)
    linear = jnp.einsum("kj,sje->ske", stiffness, corner_disp, precision=lax.Precision.HIGHEST)
    forces = (modulus * (linear + 0.25 * corner_disp * corner_disp * corner_disp)).astype(
        jnp.bfloat16
    )
    forces = forces.reshape(snaps, 3, 8, elem_count)
    matrix = jnp.einsum("cmae,scae->sme", element_basis, forces, preferred_element_type=jnp.float32)
    norm_sums = jnp.sum(jnp.sqrt(jnp.sum(matrix * matrix, axis=1)), axis=1)
    force_sums = jnp.sum(matrix, axis=2)
    norm_sums, force_sums = lax.psum((norm_sums, force_sums), ("elem", "param"))
    elem_total = elem_count * lax.axis_size("elem") * cycle_size
    row_scale = norm_sums / elem_total
    target = force_sums / (row_scale[:, None] * math.sqrt(elem_total))
    training = (matrix / row_scale[:, None, None]).astype(jnp.bfloat16)
    return (training, target)


def solution(mesh):
    in_specs = (
        P("param", None),
        P(None, None, "elem"),
        P(("elem", "param"), None),
        P(("elem", "param")),
        P(),
    )
    out_specs = (P(None, None, ("elem", "param")), P())
    return jax.shard_map(local, mesh=mesh, in_specs=in_specs, out_specs=out_specs, check_vma=False)
```

profile of v0, /device:TPU:0, one launch (start us, length us, event | category | flops | bytes accessed | tf_op | source)
XLA Modules:
  0.0 81.1 jit_solution(3763947510035681350)
XLA Ops:
  0.6 0.0 copy-start
  0.6 1.5 %copy.29 = bf16[3,300,256]{1,0,2:T(4,128)(2,1)S(1)} copy(bf16[3,300,256]{2,1,0:T(8,128)(2,1)} %param.6) | data formatting | bytes 921600 | tf_op args[1]
  2.1 0.1 slice.20
  2.2 7.0 %collective-permute-start = (bf16[3,300,64]{1,0,2:T(4,128)(2,1)S(1)}, bf16[3,300,64]{1,0,2:T(4,128)(2,1)S(1)}, u32[]{:S(2)}, u32[]{:S(2)}) collective-permute-start(bf16[3,300,64]{1,0,2:T(4,128)(2,1)S(1)} %slice.20), channel_id=1, source_target_pairs={{0,30},{2,0},{4,2},{6,4},{8,6},{10,8},{12,10},{14,12},{16,14},{18,... | collective-permute-start | bytes 345608 | tf_op jit(solution)/shard_map/ppermute | solution.py:10
  9.2 1.9 %all-gather = bf16[2,4,300]{2,1,0:T(4,128)(2,1)S(1)} all-gather(bf16[1,4,300]{2,1,0:T(4,128)(2,1)} %bitcast.72), channel_id=1, replica_groups=mesh['elem'=16,'param'=2] {'param'}, dimensions={0}, use_global_device_ids=true | all-gather | bytes 7200 | tf_op jit(solution)/shard_map/all_gather | solution.py:22
  11.2 0.7 fusion.21
  11.9 1.5 %collective-permute-done = bf16[3,300,64]{1,0,2:T(4,128)(2,1)S(1)} collective-permute-done((bf16[3,300,64]{1,0,2:T(4,128)(2,1)S(1)}, bf16[3,300,64]{1,0,2:T(4,128)(2,1)S(1)}, u32[]{:S(2)}, u32[]{:S(2)}) %collective-permute-start) | collective-permute-done | bytes 115232 | tf_op jit(solution)/shard_map/ppermute | solution.py:10
  13.4 2.1 %fusion.12 = (bf16[1,300,320]{1,0,2:T(2,128)(2,1)S(1)}, bf16[1,300,320]{1,0,2:T(2,128)(2,1)S(1)}, bf16[1,300,320]{1,0,2:T(2,128)(2,1)S(1)}) fusion(bf16[3,300,256]{1,0,2:T(4,128)(2,1)S(1)} %copy.29, bf16[3,300,64]{1,0,2:T(4,128)(2,1)S(1)} %collective-permute-done), kind=kLoop, calls=%fused_computation.28 | loop fusion | flops 288000 | bytes 1152000 | tf_op jit(solution)/shard_map/concatenate | solution.py:17
  15.5 0.0 copy-start.1
  15.5 0.9 %copy.30 = bf16[1,300,320]{2,1,0:T(8,128)(2,1)S(1)} copy(bf16[1,300,320]{1,0,2:T(2,128)(2,1)S(1)} %get-tuple-element.14) | data formatting | bytes 384000 | tf_op jit(solution)/shard_map/slice | solution.py:25
  16.3 0.9 %copy.31 = bf16[1,300,320]{2,1,0:T(8,128)(2,1)S(1)} copy(bf16[1,300,320]{1,0,2:T(2,128)(2,1)S(1)} %get-tuple-element.15) | data formatting | bytes 384000 | tf_op jit(solution)/shard_map/slice | solution.py:25
  17.2 0.1 fusion.9
  17.4 0.2 fusion.10
  17.5 0.9 %copy.32 = bf16[1,300,320]{2,1,0:T(8,128)(2,1)S(1)} copy(bf16[1,300,320]{1,0,2:T(2,128)(2,1)S(1)} %get-tuple-element.16) | data formatting | bytes 384000 | tf_op jit(solution)/shard_map/slice | solution.py:25
  18.4 0.1 fusion.11
  18.5 0.2 copy.33
  18.8 3.6 %gather_fusion = bf16[1024,8,3]{1,2,0:T(4,128)(2,1)S(1)} fusion(bf16[8,3,320]{0,1,2:T(4,128)(2,1)S(1)} %copy.33, s32[1024]{0:T(1024)S(1)} %fusion.21), kind=kCustom, calls=%fused_computation | custom fusion | bytes 102400 | tf_op jit(solution)/shard_map/gather | solution.py:31
  22.3 0.5 copy.34
  22.8 0.0 copy-done
  22.8 0.0 copy-done.1
  22.9 0.2 fusion.8
  23.0 0.4 copy.36
  23.5 0.7 pad_maximum_fusion
  24.1 9.9 %gather_fusion.1 = bf16[1024,3,300]{2,1,0:T(4,128)(2,1)} fusion(bf16[3,300,320]{1,0,2:T(4,128)(2,1)S(1)} %pad_maximum_fusion, s32[1024]{0:T(1024)S(1)} %fusion.21), kind=kCustom, calls=%fused_computation.1 | custom fusion | bytes 3690496 | tf_op jit(solution)/shard_map/gather | solution.py:20
  34.1 4.0 %bitcast_reduce_fusion = (f32[8,300]{1,0:T(8,128)S(1)}, f32[8,128]{0,1:T(8,128)S(1)}, f32[128,8,300,1]{2,1,3,0:T(8,128)S(1)}) fusion(bf16[8,3,8,128]{2,0,1,3:T(8,128)(2,1)S(1)} %copy.36, bf16[8,128,3,300]{3,2,1,0:T(4,128)(2,1)} %bitcast.71), kind=kOutput, calls=%fused_computation.5 | convolution fusion | flops 15663776 | bytes 3134848 | tf_op jit(solution)/shard_map/cmae,scae->sme/dot_general | solution.py:37
  38.1 40.7 %all-reduce = (f32[8]{0:T(128)S(1)}, f32[8,300]{1,0:T(8,128)S(1)}) all-reduce(f32[8]{0:T(128)S(1)} %sqrt_reduce_fusion, f32[8,300]{1,0:T(8,128)S(1)} %get-tuple-element.10), channel_id=1, replica_groups=mesh['elem'=16,'param'=2] {'elem','param'}, use_global_device_ids=true, to_apply=%region_2.0 | all-reduce | flops 2408 | bytes 19264 | tf_op jit(solution)/shard_map/psum | solution.py:40
  78.8 0.2 fusion.4
  79.0 1.5 %copy.37 = bf16[8,300,128]{2,0,1:T(8,128)(2,1)} copy(bf16[8,300,128]{1,0,2:T(8,128)(2,1)S(1)} %fusion.4) | data formatting | bytes 1228800
  80.5 0.7 broadcast_divide_fusion
  (4 shorter events, 0.1 us)
Async XLA Ops:
  0.6 22.2 %copy-start = (f32[24,24]{1,0:T(8,128)S(1)}, f32[24,24]{1,0:T(8,128)}, u32[]{:S(2)}) copy-start(f32[24,24]{1,0:T(8,128)} %param.9) | copy-start | bytes 6916
  2.2 11.2 %collective-permute-start = (bf16[3,300,64]{1,0,2:T(4,128)(2,1)S(1)}, bf16[3,300,64]{1,0,2:T(4,128)(2,1)S(1)}, u32[]{:S(2)}, u32[]{:S(2)}) collective-permute-start(bf16[3,300,64]{1,0,2:T(4,128)(2,1)S(1)} %slice.20), channel_id=1, source_target_pairs={{0,30},{2,0},{4,2},{6,4},{8,6},{10,8},{12,10},{14,12},{16,14},{18,... | collective-permute-start | bytes 345608 | tf_op jit(solution)/shard_map/ppermute | solution.py:10
  15.5 7.4 %copy-start.1 = (f32[128]{0:T(128)S(1)}, f32[128]{0:T(128)}, u32[]{:S(2)}) copy-start(f32[128]{0:T(128)} %param.8) | copy-start | bytes 1540
where the time goes:
time: 81.4 us; the launch traced here: 81.1 us
  blocking collectives  42.6 us (52%)
  local copies, waits for them, and re-layouts  20.2 us (25%)
  starting transfers between devices  7.01 us (9%)
  matrix products  4.58 us (6%)
  other arithmetic  4.38 us (5%)
  waiting for transfers between devices  1.51 us (2%)
    psum x1, blocking collectives, local(): norm_sums, force_sums = lax.psum((norm_sums, force_sums), ('elem', 'param'))  40.7 us
    gather x1, local copies, waits for them, and re-layouts, local(): element_basis = extended[:, :, corner_ids]  9.92 us
    ppermute x1, starting transfers between devices, passed_along(): lax.ppermute(value, axis, [(i, (i + by) % peers) for i in range(peers)])  7.01 us
    gather x2, local copies, waits for them, and re-layouts, local(): displaced[:, :, corner_ids].reshape(snaps, 24, elem_count)  4.05 us
    dot_general x1, matrix products, local(): jnp.einsum('cmae,scae->sme', element_basis, forces, preferred_element_typ...  3.98 us
    unnamed x7, local copies, waits for them, and re-layouts  2.95 us
    concatenate x2, other arithmetic, local(): extended = jnp.concatenate([basis_rows, ghost_rows], axis=2)  2.76 us
    slice x3, local copies, waits for them, and re-layouts, local(): extended[component]  2.6 us
  transfers between devices with their start and end apart: 1, of which 1 were waited for; matrix products, arithmetic and copies ran while one was open for 1% of the time, Pallas kernels for 0%

commit v1 on v0

--- a/solution.py
+++ b/solution.py
@@ -37,7 +37,7 @@
     matrix = jnp.einsum("cmae,scae->sme", element_basis, forces, preferred_element_type=jnp.float32)
     norm_sums = jnp.sum(jnp.sqrt(jnp.sum(matrix * matrix, axis=1)), axis=1)
     force_sums = jnp.sum(matrix, axis=2)
-    norm_sums, force_sums = lax.psum((norm_sums, force_sums), ("elem", "param"))
+    norm_sums, force_sums = lax.psum(lax.psum((norm_sums, force_sums), "param"), "elem")
     elem_total = elem_count * lax.axis_size("elem") * cycle_size
     row_scale = norm_sums / elem_total
     target = force_sums / (row_scale[:, None] * math.sqrt(elem_total))

time: 81.4 us -> 122 us (1.50)
  blocking collectives: 42.6 us -> 82.9 us
    psum x1 -> x2, blocking collectives: 40.7 us -> 81 us  [the longest x1 77.7 us: local(): lax.psum(lax.psum((norm_sums, force_sums), 'param'), 'elem')]
where the time goes in v1:
time: 122 us; the launch traced here: 121 us
  blocking collectives  82.9 us (68%)
  local copies, waits for them, and re-layouts  20.2 us (17%)
  starting transfers between devices  7.01 us (6%)
  matrix products  4.58 us (4%)
  other arithmetic  4.38 us (4%)
  waiting for transfers between devices  1.51 us (1%)
    psum x1, blocking collectives, local(): lax.psum(lax.psum((norm_sums, force_sums), 'param'), 'elem')  77.7 us
    gather x1, local copies, waits for them, and re-layouts, local(): element_basis = extended[:, :, corner_ids]  9.92 us
    ppermute x1, starting transfers between devices, passed_along(): lax.ppermute(value, axis, [(i, (i + by) % peers) for i in range(peers)])  7.01 us
    gather x2, local copies, waits for them, and re-layouts, local(): displaced[:, :, corner_ids].reshape(snaps, 24, elem_count)  4.05 us
    dot_general x1, matrix products, local(): jnp.einsum('cmae,scae->sme', element_basis, forces, preferred_element_typ...  3.98 us
    psum x1, blocking collectives, local(): lax.psum((norm_sums, force_sums), 'param')  3.29 us
    unnamed x7, local copies, waits for them, and re-layouts  2.95 us
    concatenate x2, other arithmetic, local(): extended = jnp.concatenate([basis_rows, ghost_rows], axis=2)  2.76 us
  transfers between devices with their start and end apart: 1, of which 1 were waited for; matrix products, arithmetic and copies ran while one was open for 1% of the time, Pallas kernels for 0%

profile of v1, /device:TPU:0, one launch (start us, length us, event | category | flops | bytes accessed | tf_op | source)
XLA Modules:
  0.0 121.4 jit_solution(5834596987355721556)
XLA Ops:
  0.6 0.0 copy-start
  0.6 1.5 %copy.29 = bf16[3,300,256]{1,0,2:T(4,128)(2,1)S(1)} copy(bf16[3,300,256]{2,1,0:T(8,128)(2,1)} %param.6) | data formatting | bytes 921600 | tf_op args[1]
  2.1 0.1 slice.20
  2.2 7.0 %collective-permute-start = (bf16[3,300,64]{1,0,2:T(4,128)(2,1)S(1)}, bf16[3,300,64]{1,0,2:T(4,128)(2,1)S(1)}, u32[]{:S(2)}, u32[]{:S(2)}) collective-permute-start(bf16[3,300,64]{1,0,2:T(4,128)(2,1)S(1)} %slice.20), channel_id=1, source_target_pairs={{0,30},{2,0},{4,2},{6,4},{8,6},{10,8},{12,10},{14,12},{16,14},{18,... | collective-permute-start | bytes 345608 | tf_op jit(solution)/shard_map/ppermute | solution.py:10
  9.2 1.9 %all-gather = bf16[2,4,300]{2,1,0:T(4,128)(2,1)S(1)} all-gather(bf16[1,4,300]{2,1,0:T(4,128)(2,1)} %bitcast.72), channel_id=1, replica_groups=mesh['elem'=16,'param'=2] {'param'}, dimensions={0}, use_global_device_ids=true | all-gather | bytes 7200 | tf_op jit(solution)/shard_map/all_gather | solution.py:22
  11.2 0.7 fusion.21
  11.9 1.5 %collective-permute-done = bf16[3,300,64]{1,0,2:T(4,128)(2,1)S(1)} collective-permute-done((bf16[3,300,64]{1,0,2:T(4,128)(2,1)S(1)}, bf16[3,300,64]{1,0,2:T(4,128)(2,1)S(1)}, u32[]{:S(2)}, u32[]{:S(2)}) %collective-permute-start) | collective-permute-done | bytes 115232 | tf_op jit(solution)/shard_map/ppermute | solution.py:10
  13.4 2.1 %fusion.12 = (bf16[1,300,320]{1,0,2:T(2,128)(2,1)S(1)}, bf16[1,300,320]{1,0,2:T(2,128)(2,1)S(1)}, bf16[1,300,320]{1,0,2:T(2,128)(2,1)S(1)}) fusion(bf16[3,300,256]{1,0,2:T(4,128)(2,1)S(1)} %copy.29, bf16[3,300,64]{1,0,2:T(4,128)(2,1)S(1)} %collective-permute-done), kind=kLoop, calls=%fused_computation.28 | loop fusion | flops 288000 | bytes 1152000 | tf_op jit(solution)/shard_map/concatenate | solution.py:17
  15.5 0.0 copy-start.1
  15.5 0.9 copy.30
  16.3 0.9 copy.31
  17.2 0.1 fusion.9
  17.4 0.2 fusion.10
  17.5 0.9 copy.32
  18.4 0.1 fusion.11
  18.5 0.2 copy.33
  18.8 3.6 %gather_fusion = bf16[1024,8,3]{1,2,0:T(4,128)(2,1)S(1)} fusion(bf16[8,3,320]{0,1,2:T(4,128)(2,1)S(1)} %copy.33, s32[1024]{0:T(1024)S(1)} %fusion.21), kind=kCustom, calls=%fused_computation | custom fusion | bytes 102400 | tf_op jit(solution)/shard_map/gather | solution.py:31
  22.3 0.5 copy.34
  22.8 0.0 copy-done
  22.8 0.0 copy-done.1
  22.9 0.2 fusion.8
  23.0 0.4 copy.36
  23.5 0.7 pad_maximum_fusion
  24.1 9.9 %gather_fusion.1 = bf16[1024,3,300]{2,1,0:T(4,128)(2,1)} fusion(bf16[3,300,320]{1,0,2:T(4,128)(2,1)S(1)} %pad_maximum_fusion, s32[1024]{0:T(1024)S(1)} %fusion.21), kind=kCustom, calls=%fused_computation.1 | custom fusion | bytes 3690496 | tf_op jit(solution)/shard_map/gather | solution.py:20
  34.1 4.0 %bitcast_reduce_fusion = (f32[8,300]{1,0:T(8,128)S(1)}, f32[8,128]{0,1:T(8,128)S(1)}, f32[128,8,300,1]{2,1,3,0:T(8,128)S(1)}) fusion(bf16[8,3,8,128]{2,0,1,3:T(8,128)(2,1)S(1)} %copy.36, bf16[8,128,3,300]{3,2,1,0:T(4,128)(2,1)} %bitcast.71), kind=kOutput, calls=%fused_computation.5 | convolution fusion | flops 15663776 | bytes 3134848 | tf_op jit(solution)/shard_map/cmae,scae->sme/dot_general | solution.py:37
  38.1 3.3 %all-reduce.1 = (f32[8]{0:T(128)S(1)}, f32[8,300]{1,0:T(8,128)S(1)}) all-reduce(f32[8]{0:T(128)S(1)} %sqrt_reduce_fusion, f32[8,300]{1,0:T(8,128)S(1)} %get-tuple-element.10), channel_id=1, replica_groups=mesh['elem'=16,'param'=2] {'param'}, use_global_device_ids=true, to_apply=%region_2.0 | all-reduce | flops 2408 | bytes 19264 | tf_op jit(solution)/shard_map/psum | solution.py:40
  41.4 77.7 %all-reduce = (f32[8]{0:T(128)S(1)}, f32[8,300]{1,0:T(8,128)S(1)}) all-reduce(f32[8]{0:T(128)S(1)} %get-tuple-element.14, f32[8,300]{1,0:T(8,128)S(1)} %get-tuple-element.15), channel_id=1, replica_groups=mesh['elem'=16,'param'=2] {'elem'}, use_global_device_ids=true, to_apply=%region_3.0 | all-reduce | flops 2408 | bytes 19264 | tf_op jit(solution)/shard_map/psum | solution.py:40
  119.1 0.2 fusion.4
  119.3 1.5 %copy.37 = bf16[8,300,128]{2,0,1:T(8,128)(2,1)} copy(bf16[8,300,128]{1,0,2:T(8,128)(2,1)S(1)} %fusion.4) | data formatting | bytes 1228800
  120.7 0.7 broadcast_divide_fusion
  (4 shorter events, 0.1 us)
Async XLA Ops:
  0.6 22.2 %copy-start = (f32[24,24]{1,0:T(8,128)S(1)}, f32[24,24]{1,0:T(8,128)}, u32[]{:S(2)}) copy-start(f32[24,24]{1,0:T(8,128)} %param.9) | copy-start | bytes 6916
  2.2 11.2 %collective-permute-start = (bf16[3,300,64]{1,0,2:T(4,128)(2,1)S(1)}, bf16[3,300,64]{1,0,2:T(4,128)(2,1)S(1)}, u32[]{:S(2)}, u32[]{:S(2)}) collective-permute-start(bf16[3,300,64]{1,0,2:T(4,128)(2,1)S(1)} %slice.20), channel_id=1, source_target_pairs={{0,30},{2,0},{4,2},{6,4},{8,6},{10,8},{12,10},{14,12},{16,14},{18,... | collective-permute-start | bytes 345608 | tf_op jit(solution)/shard_map/ppermute | solution.py:10
  15.5 7.4 %copy-start.1 = (f32[128]{0:T(128)S(1)}, f32[128]{0:T(128)}, u32[]{:S(2)}) copy-start(f32[128]{0:T(128)} %param.8) | copy-start | bytes 1540
